TPU v7x, 128 devices: a whole 4x4x4 slice. The times are simulated.
128 devices in a mesh: gx: 8 (over z, core), gy: 16 (over x, y).
Axes of the slice: x: 4, y: 4, z: 4, core: 2. Of those that a mesh axis runs over, the one named last changes fastest.
Arguments:
- prolong: bfloat16 [8192, 24, 128], P(('gx', 'gy')), may hold values from -0.5 to 0.5
- stiffness: bfloat16 [16384, 4, 128, 128], P(('gx', 'gy')), may hold values from -6 to 6
- request: int32 [16384], P(('gx', 'gy')), may hold values from 0 to 63, as said below
- col_slot: int32 [16384, 4], P(('gx', 'gy')), may hold values from 0 to 127
- col_pos: int32 [16384, 4], P(('gx', 'gy')), may hold values from 0 to 15, as said below
- coarse_owner: int32 [8192, 1], P(('gx', 'gy')), may hold values from 0 to 127; in each aligned block of 64 rows (0 to 63, 64 to 127, ...) no two rows name the same one
Outputs:
- coarse: float32 [16384, 24, 384], P(('gx', 'gy'))
Inputs may be any that keep to these rules, and one draw needn't show every extreme that they name: `request`: on each device, entries k * 1 to (k + 1) * 1 - 1 name distinct aggregates of device k, as local indices there. `col_pos`: the 4 entries of one block row are distinct. `coarse_owner`: among one device's 64 aggregates at most 1 share a coarse owner, and on some devices 1 do.
All inputs are finite; a program needn't handle non-finite values.
Results may differ from a plain program's by a relative error of at most 0.0003.
Values may be sent and summed in bfloat16 or wider, within the bound.
A program may use at most 128 MiB of HBM per device.

v0:
```python
import jax
import jax.numpy as jnp
from jax import lax
from jax.sharding import PartitionSpec as P

MAXNB = 16


HIGH = lax.Precision.HIGHEST


def side_by_side(arrays, axis, split_dim, concat_dim, along):
    columns = [a.reshape(*a.shape[:along], -1) for a in arrays]
    both = jnp.concatenate(columns, axis=along)
    result, at, done = (
        lax.all_to_all(both, axis, split_axis=split_dim, concat_axis=concat_dim, tiled=True),
        0,
        [],
    )
    for a, column in zip(arrays, columns):
        slab = result[..., at : at + column.shape[along]]
        done.append(slab.reshape(*slab.shape[:along], *a.shape[along:]))
        at += column.shape[along]
    return tuple(done)


def placed(partial_value, column_hot):
    spread = jnp.einsum("tqce,tqn->tcne", partial_value, column_hot, precision=HIGH)
    return spread.reshape(
        partial_value.shape[0], partial_value.shape[2], column_hot.shape[2] * partial_value.shape[3]
    )


def per_device(prolong, stiffness, request, col_slot, col_pos, coarse_owner):
    devices = lax.axis_size(("gx", "gy"))
    own_aggs = prolong.shape[0]
    columns = MAXNB
    requested = lax.all_to_all(request, ("gx", "gy"), split_axis=0, concat_axis=0, tiled=True)
    fetched = lax.all_to_all(
        prolong[requested], ("gx", "gy"), split_axis=0, concat_axis=0, tiled=True
    )
    col_rows = fetched[col_slot]
    applied = jnp.einsum("tqij,tqej->tqei", stiffness, col_rows, preferred_element_type=jnp.float32)
    partial_value = jnp.einsum(
        "tci,tqei->tqce", fetched.astype(jnp.float32), applied, precision=HIGH
    )
    blocks_in, where_in = side_by_side(
        (partial_value, col_pos.astype(jnp.float32)), ("gx", "gy"), 0, 0, 2
    )
    hot_in = (where_in[:, :, None] == jnp.arange(columns, dtype=jnp.float32)[None, None, :]).astype(
        jnp.float32
    )
    rows_in = placed(blocks_in, hot_in)
    owner_hot = (requested[None, :] == jnp.arange(own_aggs, dtype=jnp.int32)[:, None]).astype(
        jnp.float32
    )
    fine_rows = jnp.einsum("at,tcw->acw", owner_hot, rows_in, precision=HIGH)
    owners = coarse_owner[:, 0]
    peer_ids = jnp.arange(devices, dtype=jnp.int32)
    owner_one = (owners[:, None] == peer_ids[None, :]).astype(jnp.int32)
    before = jnp.cumsum(owner_one, axis=0) - owner_one
    row_rank = jnp.sum(before * owner_one, axis=1)
    send_max = (2 * own_aggs + devices - 1) // devices
    place_hot = (owners[None, None, :] == peer_ids[:, None, None]) & (
        row_rank[None, None, :] == jnp.arange(send_max, dtype=jnp.int32)[None, :, None]
    )
    outgoing = jnp.einsum("esa,acw->escw", place_hot.astype(jnp.float32), fine_rows, precision=HIGH)
    arrived = lax.all_to_all(outgoing, ("gx", "gy"), split_axis=0, concat_axis=0, tiled=True)
    return arrived.reshape((devices * send_max,) + fine_rows.shape[1:])


def solution(mesh):
    placed = (
        P(("gx", "gy"), None, None),
        P(("gx", "gy"), None, None, None),
        P(("gx", "gy")),
        P(("gx", "gy"), None),
        P(("gx", "gy"), None),
        P(("gx", "gy"), None),
    )
    return jax.shard_map(
        per_device,
        mesh=mesh,
        in_specs=placed,
        out_specs=P(("gx", "gy"), None, None),
        check_vma=False,
    )
```

profile of v0, /device:TPU:1, one launch (start us, length us, event | category | flops | bytes accessed | tf_op | source)
XLA Modules:
  0.0 215.7 jit_solution(2421565605549395762)
XLA Ops:
  0.0 0.0 copy-start
  0.0 0.8 copy.24
  0.8 20.9 %all_to_all.27 = s32[128,1,1]{2,1,0:T(1,128)S(1)} all-to-all(s32[128,1,1]{2,1,0:T(1,128)S(1)} %copy.24), channel_id=1, replica_groups=mesh['gx'=8,'gy'=16] {'gx','gy'}, dimensions={0} | all-to-all | bytes 1024 | tf_op jit(solution)/shard_map/all_to_all | solution.py:38
  21.7 2.3 %reduce = s32[128]{0:T(128)S(1)} reduce(s32[128,1,1]{2,1,0:T(1,128)S(1)} %all_to_all.27, s32[]{:T(128)} %constant.3.clone.1), dimensions={1,2}, to_apply=%all_to_all.18.reduce_sub_computation | reduce | bytes 1028 | tf_op jit(solution)/shard_map/all_to_all | solution.py:38
  24.1 0.0 copy-done
  24.1 1.6 gather_fusion
  25.7 4.5 %all-to-all-start.1 = ((bf16[128,24,128]{2,1,0:T(8,128)(2,1)}), bf16[128,24,128]{2,1,0:T(8,128)(2,1)S(1)}, u32[]{:S(2)}, u32[]{:S(2)}) async-start(bf16[128,24,128]{2,1,0:T(8,128)(2,1)} %gather_fusion), calls=%async_computation.1 | async-start | bytes 1572864 | tf_op jit(solution)/shard_map/all_to_all | solution.py:39
  30.2 0.7 compare_select_fusion
  30.8 0.1 copy.25
  31.0 0.1 reshape.92
  31.1 0.7 convert_element_type.5
  31.8 14.5 %all-to-all-done.1 = bf16[128,24,128]{2,1,0:T(8,128)(2,1)S(1)} async-done(((bf16[128,24,128]{2,1,0:T(8,128)(2,1)}), bf16[128,24,128]{2,1,0:T(8,128)(2,1)S(1)}, u32[]{:S(2)}, u32[]{:S(2)}) %all-to-all-start.1) | async-done | bytes 786464 | tf_op jit(solution)/shard_map/all_to_all | solution.py:39
  46.2 3.2 %gather_fusion.1 = bf16[512,24,128]{2,1,0:T(8,128)(2,1)} fusion(bf16[128,24,128]{2,1,0:T(8,128)(2,1)S(1)} %all-to-all-done.1, s32[1024]{0:T(1024)S(1)} %pad_clamp_fusion), kind=kCustom, calls=%fused_computation.1 | custom fusion | bytes 6293504 | tf_op jit(solution)/shard_map/gather | solution.py:42
  49.4 12.8 %fusion.15 = f32[128,4,24,128]{3,2,1,0:T(8,128)S(1)} fusion(bf16[128,4,24,128]{3,2,1,0:T(8,128)(2,1)} %bitcast.42, bf16[128,4,128,128]{3,2,1,0:T(8,128)(2,1)} %param.7), kind=kOutput, calls=%fused_computation.28 | convolution fusion | flops 402653184 | bytes 26214400 | tf_op jit(solution)/shard_map/tqij,tqej->tqei/dot_general | solution.py:43
  62.2 4.8 %convolution_bitcast_fusion.1 = f32[128,4,24,24]{2,3,1,0:T(8,128)} fusion(f32[128,4,24,128]{3,2,1,0:T(8,128)S(1)} %fusion.15, bf16[128,24,128]{2,1,0:T(8,128)(2,1)S(1)} %all-to-all-done.1), kind=kOutput, calls=%fused_computation.3 | convolution fusion | flops 452984832 | bytes 8257536 | tf_op jit(solution)/shard_map/tci,tqei->tqce/dot_general | solution.py:44
  67.0 5.5 %copy.26 = f32[128,4,24,24]{0,3,2,1:T(8,128)S(1)} copy(f32[128,4,24,24]{2,3,1,0:T(8,128)} %convolution_bitcast_fusion.1) | data formatting | bytes 2359296 | tf_op jit(solution)/shard_map/tci,tqei->tqce/transpose | solution.py:44
  72.4 0.0 copy-start.2
  72.4 0.1 pad_maximum_fusion
  72.5 1.5 copy.27
  74.0 4.8 %all-to-all-start.2 = ((f32[128,4,577]{2,1,0:T(4,128)}), f32[128,4,577]{2,1,0:T(4,128)S(1)}, u32[]{:S(2)}, u32[]{:S(2)}) async-start(f32[128,4,577]{2,1,0:T(4,128)} %copy.27), calls=%async_computation.2 | async-start | bytes 2621440 | tf_op jit(solution)/shard_map/all_to_all | solution.py:16
  78.9 0.0 copy-done.2
  78.9 0.1 fusion.4
  78.9 0.1 reduce_window_sum.11
  79.0 0.2 select_reduce_fusion
  79.2 21.1 %all-to-all-done.2 = f32[128,4,577]{2,1,0:T(4,128)S(1)} async-done(((f32[128,4,577]{2,1,0:T(4,128)}), f32[128,4,577]{2,1,0:T(4,128)S(1)}, u32[]{:S(2)}, u32[]{:S(2)}) %all-to-all-start.2) | async-done | bytes 1181728 | tf_op jit(solution)/shard_map/all_to_all | solution.py:16
  100.3 0.9 copy.38
  101.2 4.6 %copy.31 = f32[128,4,24,24]{3,1,2,0:T(4,128)} copy(f32[128,4,24,24]{0,3,2,1:T(8,128)S(1)} %bitcast.47) | data formatting | bytes 2359296 | tf_op jit(solution)/shard_map/reshape | solution.py:22
  105.8 0.2 slice.12
  106.0 0.1 copy.28
  106.1 0.1 copy.29
  106.3 19.0 %convolution_bitcast_fusion = f32[128,24,16,24]{3,2,1,0:T(8,128)} fusion(f32[128,4,24,24]{3,1,2,0:T(4,128)} %copy.31, f32[128,4]{1,0:T(8,128)S(1)} %copy.29), kind=kOutput, calls=%fused_computation.2 | convolution fusion | flops 56631296 | bytes 5900288 | tf_op jit(solution)/shard_map/tqce,tqn->tcne/dot_general | solution.py:28
  125.3 15.4 %copy.32 = f32[128,24,16,24]{0,3,2,1:T(8,128)} copy(f32[128,24,16,24]{3,2,1,0:T(8,128)} %convolution_bitcast_fusion) | data formatting | bytes 9437184 | tf_op jit(solution)/shard_map/tqce,tqn->tcne/transpose | solution.py:28
  140.7 5.2 %fusion.9 = f32[64,24,384]{2,0,1:T(8,128)S(1)} fusion(f32[128,24,384]{0,2,1:T(8,128)} %bitcast.43, s32[128]{0:T(128)S(1)} %reduce), kind=kOutput, calls=%fused_computation.18 | convolution fusion | flops 905977856 | bytes 7078400 | tf_op jit(solution)/shard_map/at,tcw->acw/dot_general | solution.py:57
  145.9 2.1 convolution_bitcast_fusion.2
  148.1 2.7 %copy.34 = f32[128,1,24,384]{3,2,1,0:T(8,128)S(1)} copy(f32[128,1,24,384]{3,0,2,1:T(8,128)S(1)} %convolution_bitcast_fusion.2) | data formatting | bytes 9437184 | tf_op jit(solution)/shard_map/esa,acw->escw/dot_general | solution.py:67
  150.8 62.7 %all_to_all.28 = f32[128,1,24,384]{3,2,1,0:T(8,128)S(1)} all-to-all(f32[128,1,24,384]{3,2,1,0:T(8,128)S(1)} %copy.34), channel_id=1, replica_groups=mesh['gx'=8,'gy'=16] {'gx','gy'}, dimensions={0} | all-to-all | bytes 9437184 | tf_op jit(solution)/shard_map/all_to_all | solution.py:68
  213.5 0.0 copy-start.1
  213.5 2.2 %copy.40 = f32[128,24,384]{2,1,0:T(8,128)} copy(f32[128,24,384]{2,1,0:T(8,128)S(1)} %bitcast.44) | data formatting | bytes 9437184
  215.7 0.0 copy-done.1
  (4 shorter events, 0.0 us)
Async XLA Ops:
  0.0 24.1 %copy-start = (bf16[64,24,128]{2,1,0:T(8,128)(2,1)S(1)}, bf16[64,24,128]{2,1,0:T(8,128)(2,1)}, u32[]{:S(2)}) copy-start(bf16[64,24,128]{2,1,0:T(8,128)(2,1)} %param.6) | copy-start | bytes 1179652
  25.7 20.5 %all-to-all-start.1 = ((bf16[128,24,128]{2,1,0:T(8,128)(2,1)}), bf16[128,24,128]{2,1,0:T(8,128)(2,1)S(1)}, u32[]{:S(2)}, u32[]{:S(2)}) async-start(bf16[128,24,128]{2,1,0:T(8,128)(2,1)} %gather_fusion), calls=%async_computation.1 | async-start | bytes 1572864 | tf_op jit(solution)/shard_map/all_to_all | solution.py:39
  72.4 6.4 %copy-start.2 = (s32[64,1]{0,1:T(1,128)S(1)}, s32[64,1]{0,1:T(1,128)}, u32[]{:S(2)}) copy-start(s32[64,1]{0,1:T(1,128)} %param.11) | copy-start | bytes 772
  74.0 26.2 %all-to-all-start.2 = ((f32[128,4,577]{2,1,0:T(4,128)}), f32[128,4,577]{2,1,0:T(4,128)S(1)}, u32[]{:S(2)}, u32[]{:S(2)}) async-start(f32[128,4,577]{2,1,0:T(4,128)} %copy.27), calls=%async_computation.2 | async-start | bytes 2621440 | tf_op jit(solution)/shard_map/all_to_all | solution.py:16
  213.5 2.2 %copy-start.1 = (bf16[64,24,128]{2,1,0:T(8,128)(2,1)S(1)}, bf16[64,24,128]{2,1,0:T(8,128)(2,1)}, u32[]{:S(2)}) copy-start(bf16[64,24,128]{2,1,0:T(8,128)(2,1)} %param.6) | copy-start | bytes 1179652
where the time goes:
time: 216 us
  blocking collectives  83.6 us (39%)
  matrix products  44 us (20%)
  local copies, waits for them, and re-layouts  39 us (18%)
  waiting for transfers between devices  35.5 us (16%)
  starting transfers between devices  9.28 us (4%)
  other arithmetic  4.17 us (2%)
    all_to_all x1, blocking collectives, per_device(): lax.all_to_all(outgoing, ('gx', 'gy'), split_axis=0, concat_axis=0, tiled...  62.7 us
    all_to_all x1, waiting for transfers between devices, side_by_side(): lax.all_to_all(both, axis, split_axis=split_dim, concat_axis=concat_dim,...  21.1 us
    all_to_all x1, blocking collectives, per_device(): lax.all_to_all(request, ('gx', 'gy'), split_axis=0, concat_axis=0, tiled=...  20.9 us
    dot_general x1, matrix products, placed(): jnp.einsum('tqce,tqn->tcne', partial_value, column_hot, precision=HIGH)  19 us
    transpose x1, local copies, waits for them, and re-layouts, placed(): jnp.einsum('tqce,tqn->tcne', partial_value, column_hot, precision=HIGH)  15.4 us
    all_to_all x1, waiting for transfers between devices, per_device(): lax.all_to_all(prolong[requested], ('gx', 'gy'), split_axis=0, concat_axi...  14.5 us
    dot_general x1, matrix products, per_device(): jnp.einsum('tqij,tqej->tqei', stiffness, col_rows, preferred_element_type...  12.8 us
    transpose x1, local copies, waits for them, and re-layouts, per_device(): jnp.einsum('tci,tqei->tqce', fetched.astype(jnp.float32), applied, precis...  5.46 us
  transfers between devices with their start and end apart: 2, of which 2 were waited for; matrix products, arithmetic and copies ran while one was open for 1% of the time, Pallas kernels for 0%

commit v1 on v0

v1 whole, which is shorter than its diff:
```python
import functools

import jax
import jax.numpy as jnp
from jax import lax
from jax.experimental import pallas as pl
from jax.experimental.pallas import tpu as pltpu
from jax.sharding import PartitionSpec as P

MESH = pl.DeviceIdType.MESH
STRIDE = 37
LEVELS = 32766.0
FLOOR = 1e-30
CHUNK = 16


def neighbour(s, gx, gy):
    o = lax.rem(s * STRIDE, 128)
    z, core, x, y = gx // 2, gx % 2, gy // 4, gy % 4
    z = (z + o // 32) % 4
    core = (core + (o // 16) % 2) % 2
    x = (x + (o // 4) % 4) % 4
    y = (y + o % 4) % 4
    tx, ty = z * 2 + core, x * 4 + y
    return {"gx": tx, "gy": ty}, tx * 16 + ty


def wait_all(ref, rows, sem):
    part = ref.at[pl.ds(0, rows)]
    pltpu.make_async_copy(part, part, sem).wait()


def exchange_kernel(
    request, slot_of, pos_of, owner_b, prolong, stiffness,
    arrived, scales,
    kbuf, ask, asked, asked_s, stage, fetched_in, fetched, payload, partial_in,
    plan, plan_s, running, outgoing, outscale,
    ksem, local, send, recv,
):
    devices = 128
    gx, gy = lax.axis_index("gx"), lax.axis_index("gy")
    me = gx * 16 + gy
    rows, width = payload.shape[1], payload.shape[2]
    cols = outgoing.shape[2]

    kcopies = [
        pltpu.make_async_copy(
            stiffness.at[pl.ds(c * CHUNK, CHUNK)], kbuf.at[pl.ds(c * CHUNK, CHUNK)], ksem.at[c]
        )
        for c in range(devices // CHUNK)
    ]
    for copy in kcopies:
        copy.start()

    barrier = pltpu.get_barrier_semaphore()

    @pl.loop(1, devices)
    def _(s):
        there, _ = neighbour(s, gx, gy)
        pl.semaphore_signal(barrier, inc=1, device_id=there, device_id_type=MESH)

    lane1 = lax.broadcasted_iota(jnp.int32, (1, 128), 1)

    @pl.loop(0, devices)
    def _(t):
        row = jnp.where(lane1 == 0, request[t], 0)
        for q in range(4):
            row = jnp.where(lane1 == q + 1, pos_of[q, t], row)
        ask[t] = row

    pl.semaphore_wait(barrier, devices - 1)

    def exchange(source, target, phase, lo=1, hi=devices):
        @pl.loop(lo, hi)
        def _(s):
            there, t = neighbour(s, gx, gy)
            pltpu.make_async_remote_copy(
                src_ref=source.at[t],
                dst_ref=target.at[me],
                send_sem=send.at[phase],
                recv_sem=recv.at[phase],
                device_id=there,
                device_id_type=MESH,
            ).start()

    def keep(source, target):
        copy = pltpu.make_async_copy(source.at[me], target.at[me], local)
        copy.start()
        copy.wait()

    exchange(ask, asked, 0)
    keep(ask, asked)
    wait_all(asked, devices - 1, recv.at[0])
    to_scalars = pltpu.make_async_copy(asked, asked_s, local)
    to_scalars.start()
    to_scalars.wait()

    @pl.loop(0, devices, unroll=4)
    def _(d):
        stage[d] = prolong[asked_s[d, 0, 0]]

    exchange(stage, fetched_in, 1)
    keep(stage, fetched_in)

    table = asked[...].reshape(devices, 128)
    wanted = jnp.transpose(table)[0:1, :]
    agg = lax.broadcasted_iota(jnp.int32, owner_b.shape, 0)
    goes_to = jnp.sum(jnp.where(agg == wanted, owner_b[...], 0), axis=0, keepdims=True)
    lane = lax.broadcasted_iota(jnp.int32, (devices, 128), 1)
    sub = lax.broadcasted_iota(jnp.int32, (devices, 128), 0)
    key_lane = jnp.broadcast_to(goes_to * 128 + lane1, (devices, 128))
    key_sub = jnp.transpose(key_lane)
    rank = jnp.sum((key_sub < key_lane).astype(jnp.int32), axis=0, keepdims=True)
    rank_sub = jnp.transpose(jnp.broadcast_to(rank, (devices, 128)))
    owner_sub = key_sub // 128
    here = rank_sub == lane
    order = jnp.sum(jnp.where(here, sub, 0), axis=0, keepdims=True)
    sorted_owner = jnp.sum(jnp.where(here, owner_sub, 0), axis=0, keepdims=True)
    before = pltpu.roll(sorted_owner, 1, 1)
    same = jnp.where(lane1 == 0, 0, (sorted_owner == before).astype(jnp.int32))
    up_to = jnp.sum((owner_sub <= lane).astype(jnp.int32), axis=0, keepdims=True)
    count = jnp.sum((owner_sub == lane).astype(jnp.int32), axis=0, keepdims=True)
    plan[0:1, :] = order
    plan[1:2, :] = same
    plan[2:3, :] = jnp.maximum(up_to - 1, 0)
    plan[3:4, :] = jnp.minimum(count, 1)
    to_scalars = pltpu.make_async_copy(plan, plan_s, local)
    to_scalars.start()
    to_scalars.wait()

    wait_all(fetched_in, devices - 1, recv.at[1])

    @pl.loop(0, devices, unroll=4)
    def _(t):
        fetched[t] = fetched_in[t].astype(jnp.float32)

    for copy in kcopies:
        copy.wait()

    lane_p = lax.broadcasted_iota(jnp.int32, (rows, width), 1)

    def triple(s):
        _, t = neighbour(s, gx, gy)
        p = fetched[t].astype(jnp.bfloat16)
        pieces, columns = [], []
        for q in range(4):
            pk = jnp.dot(p, kbuf[t, q], preferred_element_type=jnp.float32)
            high = pk.astype(jnp.bfloat16).astype(jnp.float32)
            pieces += [high, pk - high]
            columns.append(fetched[slot_of[q, t]])
        left = jnp.concatenate(pieces, axis=0).astype(jnp.bfloat16)
        right = jnp.concatenate(columns + [jnp.zeros((32, 128), jnp.float32)], axis=0).astype(jnp.bfloat16)
        both = lax.dot_general(
            left, right, (((1,), (1,)), ((), ())), preferred_element_type=jnp.float32
        )
        value = jnp.zeros((rows, width), jnp.float32)
        for q in range(4):
            mine = both[2 * q * rows : (2 * q + 1) * rows] + both[(2 * q + 1) * rows : (2 * q + 2) * rows]
            value = jnp.where((lane_p >= 24 * q) & (lane_p < 24 * (q + 1)), mine, value)
        top = jnp.maximum(jnp.max(jnp.abs(value), axis=1, keepdims=True), FLOOR)
        power = jnp.floor(jnp.log2(top)) + 1.0
        coded = jnp.clip(jnp.round(value * jnp.exp2(15.0 - power)), -32767.0, 32767.0)
        coded = jnp.where(lane_p >= 96, power, coded)
        payload[t] = coded.astype(jnp.int32).astype(jnp.int16)

    for c in range(devices // CHUNK):
        @pl.loop(c * CHUNK, (c + 1) * CHUNK, unroll=4)
        def _(s):
            triple(s)

        if c:
            exchange(payload, partial_in, 2, max(1, (c - 1) * CHUNK), c * CHUNK)
    exchange(payload, partial_in, 2, devices - CHUNK, devices)
    keep(payload, partial_in)
    wait_all(partial_in, devices - 1, recv.at[2])

    lanes = [lax.broadcasted_iota(jnp.int32, (rows, 128), 1) + 128 * j for j in range(cols // 128)]
    column = [l // 24 for l in lanes]
    within = [l % 24 for l in lanes]

    def add(i, carry):
        d = plan_s[0, i]
        joined = plan_s[1, i].astype(jnp.float32)
        got = partial_in[d].astype(jnp.int32).astype(jnp.float32)
        scale = jnp.exp2(got[:, 96:97] - 15.0)
        value = got * scale
        result = []
        for j in range(cols // 128):
            index = jnp.zeros((rows, 128), jnp.int32)
            hit = jnp.zeros((rows, 128), jnp.bool_)
            for q in range(4):
                eq = column[j] == asked_s[d, 0, q + 1]
                index = jnp.where(eq, within[j] + 24 * q, index)
                hit = hit | eq
            moved = jnp.take_along_axis(value, index, axis=1)
            total = carry[j] * joined + jnp.where(hit, moved, 0.0)
            running[i, :, 128 * j : 128 * (j + 1)] = total
            result.append(total)
        return tuple(result)

    zero = jnp.zeros((rows, 128), jnp.float32)
    lax.fori_loop(0, devices, add, (zero,) * (cols // 128), unroll=2)

    diagonal = lax.broadcasted_iota(jnp.int32, (rows, 128), 1) == lax.broadcasted_iota(
        jnp.int32, (rows, 128), 0
    )

    def encode(s):
        _, t = neighbour(s, gx, gy)
        value = running[plan_s[2, t]] * plan_s[3, t].astype(jnp.float32)
        top = jnp.maximum(jnp.max(jnp.abs(value), axis=1, keepdims=True), FLOOR)
        coded = jnp.round(value * (LEVELS / top))
        outgoing[t] = coded.astype(jnp.int32).astype(jnp.int16)
        outscale[t] = jnp.sum(jnp.where(diagonal, top * (1.0 / LEVELS), 0.0), axis=0, keepdims=True)

    for c in range(devices // CHUNK):
        @pl.loop(c * CHUNK, (c + 1) * CHUNK, unroll=2)
        def _(s):
            encode(s)

        if c:
            exchange(outgoing, arrived, 3, max(1, (c - 1) * CHUNK), c * CHUNK)
    exchange(outgoing, arrived, 3, devices - CHUNK, devices)
    exchange(outscale, scales, 4)
    keep(outgoing, arrived)
    keep(outscale, scales)

    wait_all(ask, devices - 1, send.at[0])
    wait_all(stage, devices - 1, send.at[1])
    wait_all(payload, devices - 1, send.at[2])
    wait_all(outgoing, devices - 1, send.at[3])
    wait_all(outscale, devices - 1, send.at[4])
    wait_all(arrived, devices - 1, recv.at[3])
    wait_all(scales, devices - 1, recv.at[4])


def decode_kernel(arrived, scales, out):
    rows, cols = out.shape[1], out.shape[2]
    diagonal = lax.broadcasted_iota(jnp.int32, (rows, 128), 1) == lax.broadcasted_iota(
        jnp.int32, (rows, 128), 0
    )

    @pl.loop(0, out.shape[0], unroll=4)
    def _(i):
        scale = jnp.sum(jnp.where(diagonal, scales[i], 0.0), axis=1, keepdims=True)
        out[i] = arrived[i].astype(jnp.int32).astype(jnp.float32) * scale


def per_device(prolong, stiffness, request, col_slot, col_pos, coarse_owner):
    slots, per_row, dof, _ = stiffness.shape
    vectors = prolong.shape[1]
    cols = 16 * vectors
    vmem = pl.BlockSpec(memory_space=pltpu.VMEM)
    smem = pl.BlockSpec(memory_space=pltpu.SMEM)
    owner_b = jnp.broadcast_to(coarse_owner, (coarse_owner.shape[0], 128))
    arrived, scales = pl.pallas_call(
        exchange_kernel,
        out_shape=(
            jax.ShapeDtypeStruct((slots, vectors, cols), jnp.int16),
            jax.ShapeDtypeStruct((slots, 1, 128), jnp.float32),
        ),
        in_specs=[smem, smem, smem, vmem, vmem, pl.BlockSpec(memory_space=pl.ANY)],
        out_specs=(vmem, vmem),
        scratch_shapes=[
            pltpu.VMEM((slots, per_row, dof, dof), jnp.bfloat16),
            pltpu.VMEM((slots, 1, 128), jnp.int32),
            pltpu.VMEM((slots, 1, 128), jnp.int32),
            pltpu.SMEM((slots, 1, 128), jnp.int32),
            pltpu.VMEM((slots, vectors, dof), jnp.bfloat16),
            pltpu.VMEM((slots, vectors, dof), jnp.bfloat16),
            pltpu.VMEM((slots, vectors, dof), jnp.float32),
            pltpu.VMEM((slots, vectors, 128), jnp.int16),
            pltpu.VMEM((slots, vectors, 128), jnp.int16),
            pltpu.VMEM((8, 128), jnp.int32),
            pltpu.SMEM((8, 128), jnp.int32),
            pltpu.VMEM((slots, vectors, cols), jnp.float32),
            pltpu.VMEM((slots, vectors, cols), jnp.int16),
            pltpu.VMEM((slots, 1, 128), jnp.float32),
            pltpu.SemaphoreType.DMA((slots // CHUNK,)),
            pltpu.SemaphoreType.DMA,
            pltpu.SemaphoreType.DMA((5,)),
            pltpu.SemaphoreType.DMA((5,)),
        ],
        compiler_params=pltpu.CompilerParams(
            collective_id=0, has_side_effects=True, vmem_limit_bytes=60 * 1024 * 1024
        ),
        name="galerkin_exchange",
    )(request, col_slot.T, col_pos.T, owner_b, prolong, stiffness)
    step = CHUNK
    return pl.pallas_call(
        decode_kernel,
        out_shape=jax.ShapeDtypeStruct((slots, vectors, cols), jnp.float32),
        grid=(slots // step,),
        in_specs=[
            pl.BlockSpec((step, vectors, cols), lambda i: (i, 0, 0)),
            pl.BlockSpec((step, 1, 128), lambda i: (i, 0, 0)),
        ],
        out_specs=pl.BlockSpec((step, vectors, cols), lambda i: (i, 0, 0)),
        name="decode",
    )(arrived, scales)


def solution(mesh):
    placed = (
        P(("gx", "gy"), None, None),
        P(("gx", "gy"), None, None, None),
        P(("gx", "gy")),
        P(("gx", "gy"), None),
        P(("gx", "gy"), None),
        P(("gx", "gy"), None),
    )
    return jax.shard_map(
        per_device,
        mesh=mesh,
        in_specs=placed,
        out_specs=P(("gx", "gy"), None, None),
        check_vma=False,
    )
```

time: 216 us -> 131 us (0.61)
  Pallas kernels: 0 us -> 129 us
  blocking collectives: 83.6 us -> 0 us
  matrix products: 44 us -> 0 us
  local copies, waits for them, and re-layouts: 39 us -> 1.34 us
  waiting for transfers between devices: 35.5 us -> 0 us
  starting transfers between devices: 9.28 us -> 0 us
  other arithmetic: 4.17 us -> 0 us
    pallas_call x0 -> x2, Pallas kernels: none -> 129 us  [the longest x1 122 us: per_device(): pl.pallas_call(exchange_kernel, out_shape=(jax.ShapeDtypeStruct((slots, v...]
    all_to_all x2 -> x0, blocking collectives: 83.6 us -> none  [the longest x1 62.7 us: per_device(): lax.all_to_all(outgoing, ('gx', 'gy'), split_axis=0, concat_axis=0, tiled...]
    dot_general x5 -> x0, matrix products: 44 us -> none  [the longest x1 19 us: placed(): jnp.einsum('tqce,tqn->tcne', partial_value, column_hot, precision=HIGH)]
    all_to_all x2 -> x0, waiting for transfers between devices: 35.5 us -> none  [the longest x1 21.1 us: side_by_side(): lax.all_to_all(both, axis, split_axis=split_dim, concat_axis=concat_dim,...]
    transpose x2 -> x0, local copies, waits for them, and re-layouts: 20.9 us -> none  [the longest x1 15.4 us: placed(): jnp.einsum('tqce,tqn->tcne', partial_value, column_hot, precision=HIGH)]
    all_to_all x2 -> x0, starting transfers between devices: 9.28 us -> none  [the longest x1 4.8 us: side_by_side(): lax.all_to_all(both, axis, split_axis=split_dim, concat_axis=concat_dim,...]
    gather x2 -> x0, local copies, waits for them, and re-layouts: 4.73 us -> none  [the longest x1 3.15 us: per_device(): col_rows = fetched[col_slot]]
    reshape x1 -> x0, local copies, waits for them, and re-layouts: 4.64 us -> none  [side_by_side(): done.append(slab.reshape(*slab.shape[:along], *a.shape[along:]))]
  transfers between devices with their start and end apart: 2 -> 0, of which waited for: 2 -> 0; matrix products, arithmetic and copies ran while one was open for 1% -> 0% of each run, Pallas kernels for 0% -> 0%
where the time goes in v1:
time: 131 us
  Pallas kernels  129 us (98%)
  local copies, waits for them, and re-layouts  1.34 us (1%)
    pallas_call x1, Pallas kernels, per_device(): pl.pallas_call(exchange_kernel, out_shape=(jax.ShapeDtypeStruct((slots, v...  122 us
    pallas_call x1, Pallas kernels, per_device(): pl.pallas_call(decode_kernel, out_shape=jax.ShapeDtypeStruct((slots, vect...  7.42 us

profile of v1, /device:TPU:1, one launch (start us, length us, event | category | flops | bytes accessed | tf_op | source)
XLA Modules:
  0.0 130.6 jit_solution(7014305508900097377)
XLA Ops:
  0.0 1.3 %broadcast_in_dim.8.owner_b = s32[64,128]{1,0:T(8,128)} broadcast(s32[64]{0:T(128)} %bitcast.5), dimensions={0} | broadcast | bytes 33024 | tf_op jit(solution)/shard_map/broadcast_in_dim | solution.py:255
  1.3 121.9 %galerkin_exchange.1 = (s16[128,24,384]{2,1,0:T(8,128)(2,1)}, f32[128,1,128]{2,1,0:T(1,128)}) custom-call(s32[128]{0:T(128)} %request.1, s32[4,128]{1,0:T(4,128)} %bitcast.3, s32[4,128]{1,0:T(4,128)} %bitcast.4, s32[64,128]{1,0:T(8,128)} %broadcast_in_dim.8.owner_b, bf16[64,24,128]{2,1,0:T(8,128)(2,1)} %prolong.1, bf16[128,4,128,128]{3,2,1,0:T(8,128)(2,1)} %stiffness.1), custom_call_target="tpu_custom_call" | custom-call | tf_op jit(solution)/shard_map/galerkin_exchange/pallas_call | solution.py:256
  123.2 7.4 %decode.1 = f32[128,24,384]{2,1,0:T(8,128)} custom-call(s16[128,24,384]{2,1,0:T(8,128)(2,1)} %get-tuple-element.7.arrived, f32[128,1,128]{2,1,0:T(1,128)} %get-tuple-element.8.scales), custom_call_target="tpu_custom_call" | custom-call | tf_op jit(solution)/shard_map/decode/pallas_call | solution.py:290

commit v2 on v1

v2 whole, which is shorter than its diff:
```python
import jax
import jax.numpy as jnp
from jax import lax
from jax.experimental import pallas as pl
from jax.experimental.pallas import tpu as pltpu
from jax.sharding import PartitionSpec as P

MESH = pl.DeviceIdType.MESH
DEVICES = 128
STRIDE = 37
LEVELS = 32766.0
FLOOR = 1e-30
GROUP = 16
LAG = 2
TOP, LOW = 0b1011010, 0b0100101


def plus(me, s):
    o = (s * STRIDE) & (DEVICES - 1)
    return ((me & LOW) + (o & LOW)) ^ ((me ^ o) & TOP)


def minus(me, s):
    o = (s * STRIDE) & (DEVICES - 1)
    return ((me | TOP) - (o & LOW)) ^ ((me ^ ~o) & TOP)


def there(t):
    return {"gx": t >> 4, "gy": t & 15}


def wait_rows(ref, rows, sem):
    part = ref.at[pl.ds(0, rows)]
    pltpu.make_async_copy(part, part, sem).wait()


def exchange_kernel(
    request, slot_of, pos_of, owner_row, prolong, stiffness,
    arrived, scales,
    kbuf, ask, asked, table, table_s, stage, fetched_in, fetched, firsts, payload, partial_in,
    plan, plan_s, running, outgoing, outscale,
    ksem, local, send, recv, recv_block,
):
    me = lax.axis_index("gx") * 16 + lax.axis_index("gy")
    rows, width = payload.shape[1], payload.shape[2]
    cols = outgoing.shape[2]
    others = DEVICES - 1

    kcopy = pltpu.make_async_copy(stiffness, kbuf, ksem)
    kcopy.start()

    barrier = pltpu.get_barrier_semaphore()

    @pl.loop(1, DEVICES)
    def _(s):
        pl.semaphore_signal(barrier, inc=1, device_id=there(plus(me, s)), device_id_type=MESH)

    lane1 = lax.broadcasted_iota(jnp.int32, (1, 128), 1)

    @pl.loop(0, DEVICES, unroll=4)
    def _(t):
        row = jnp.where(lane1 == 0, request[t], 0)
        for q in range(4):
            row = jnp.where(lane1 == q + 1, pos_of[q, t], row)
        ask[t] = row

    pl.semaphore_wait(barrier, others)

    def push(source, target, t, send_sem, recv_sem):
        pltpu.make_async_remote_copy(
            src_ref=source.at[t],
            dst_ref=target.at[me],
            send_sem=send_sem,
            recv_sem=recv_sem,
            device_id=there(t),
            device_id_type=MESH,
        ).start()

    def keep(source, target, sem):
        pltpu.make_async_copy(source.at[me], target.at[me], sem).start()

    @pl.loop(1, DEVICES)
    def _(s):
        push(ask, asked, plus(me, s), send.at[0], recv.at[0])

    keep(ask, asked, recv.at[0])
    wait_rows(asked, DEVICES, recv.at[0])
    asks = jnp.transpose(asked[...].reshape(DEVICES, 128))
    table[...] = asks[0:8, :]
    to_scalars = pltpu.make_async_copy(table, table_s, local.at[0])
    to_scalars.start()
    to_scalars.wait()

    @pl.loop(0, DEVICES, unroll=8)
    def _(d):
        stage[d] = prolong[table_s[0, d]]

    @pl.loop(1, DEVICES)
    def _(s):
        push(stage, fetched_in, plus(me, s), send.at[1], recv_block.at[(s - 1) >> 4])

    keep(stage, fetched_in, recv_block.at[DEVICES // GROUP - 1])

    wanted = asks[0:1, :]
    own = jnp.transpose(jnp.broadcast_to(owner_row[...], (128, owner_row.shape[1])))
    agg = lax.broadcasted_iota(jnp.int32, own.shape, 0)
    goes_to = jnp.sum(jnp.where(agg == wanted, own, 0), axis=0, keepdims=True)
    lane = lax.broadcasted_iota(jnp.int32, (DEVICES, 128), 1)
    sub = lax.broadcasted_iota(jnp.int32, (DEVICES, 128), 0)
    key_lane = jnp.broadcast_to(goes_to * 128 + lane1, (DEVICES, 128))
    key_sub = jnp.transpose(key_lane)
    rank = jnp.sum((key_sub < key_lane).astype(jnp.int32), axis=0, keepdims=True)
    rank_sub = jnp.transpose(jnp.broadcast_to(rank, (DEVICES, 128)))
    owner_sub = key_sub >> 7
    here = rank_sub == lane
    order = jnp.sum(jnp.where(here, sub, 0), axis=0, keepdims=True)
    sorted_owner = jnp.sum(jnp.where(here, owner_sub, 0), axis=0, keepdims=True)
    before = pltpu.roll(sorted_owner, 1, 1)
    same = jnp.where(lane1 == 0, 0, (sorted_owner == before).astype(jnp.int32))
    up_to = jnp.sum((owner_sub <= lane).astype(jnp.int32), axis=0, keepdims=True)
    count = jnp.sum((owner_sub == lane).astype(jnp.int32), axis=0, keepdims=True)
    plan[0:1, :] = order
    plan[1:2, :] = same
    plan[2:3, :] = jnp.maximum(up_to - 1, 0)
    plan[3:4, :] = jnp.minimum(count, 1)
    plan_copy = pltpu.make_async_copy(plan, plan_s, local.at[1])
    plan_copy.start()

    kcopy.wait()

    @pl.loop(0, DEVICES // GROUP)
    def _(g):
        wait_rows(fetched_in, GROUP, recv_block.at[g])

        @pl.loop(0, GROUP, unroll=4)
        def _(i):
            t = minus(me, g * GROUP + i + 1)
            p = fetched_in[t]
            fetched[t] = p.astype(jnp.float32)
            pieces = []
            for q in range(4):
                pk = jnp.dot(p, kbuf[t, q], preferred_element_type=jnp.float32)
                high = pk.astype(jnp.bfloat16).astype(jnp.float32)
                pieces += [high, pk - high]
            firsts[t] = jnp.concatenate(pieces, axis=0).astype(jnp.bfloat16)

    lane_p = lax.broadcasted_iota(jnp.int32, (rows, width), 1)

    def second(s):
        t = plus(me, s)
        columns = [fetched[slot_of[q, t]] for q in range(4)]
        right = jnp.concatenate(columns + [jnp.zeros((32, 128), jnp.float32)], axis=0).astype(jnp.bfloat16)
        both = lax.dot_general(
            firsts[t], right, (((1,), (1,)), ((), ())), preferred_element_type=jnp.float32
        )
        value = jnp.zeros((rows, width), jnp.float32)
        for q in range(4):
            mine = both[2 * q * rows : (2 * q + 1) * rows] + both[(2 * q + 1) * rows : (2 * q + 2) * rows]
            value = jnp.where((lane_p >= 24 * q) & (lane_p < 24 * (q + 1)), mine, value)
        top = jnp.maximum(jnp.max(jnp.abs(value), axis=1, keepdims=True), FLOOR)
        power = jnp.floor(jnp.log2(top)) + 1.0
        coded = jnp.round(value * (jnp.exp2(-power) * LEVELS))
        coded = jnp.where(lane_p >= 96, power, coded)
        payload[t] = coded.astype(jnp.int32).astype(jnp.int16)

    def pipelined(make, post):
        @pl.loop(0, LAG)
        def _(g):
            for j in range(4):
                make(4 * g + j + 1)

        @pl.loop(LAG, DEVICES // 4)
        def _(g):
            for j in range(4):
                make(4 * g + j + 1)
            for j in range(4):
                post(4 * (g - LAG) + j + 1)

        @pl.loop(4 * (DEVICES // 4 - LAG) + 1, DEVICES)
        def _(s):
            post(s)

    pipelined(second, lambda s: push(payload, partial_in, plus(me, s), send.at[2], recv.at[1]))
    keep(payload, partial_in, recv.at[1])
    plan_copy.wait()
    wait_rows(partial_in, DEVICES, recv.at[1])

    lanes = [lax.broadcasted_iota(jnp.int32, (rows, 128), 1) + 128 * j for j in range(cols // 128)]
    column = [l // 24 for l in lanes]
    within = [l % 24 for l in lanes]
    blocks = cols // 128

    def spread(i):
        d = plan_s[0, i]
        got = partial_in[d].astype(jnp.int32).astype(jnp.float32)
        value = got * (jnp.exp2(got[:, 96:97]) * (1.0 / LEVELS))
        result = []
        for j in range(blocks):
            index = jnp.zeros((rows, 128), jnp.int32)
            hit = jnp.zeros((rows, 128), jnp.bool_)
            for q in range(4):
                eq = column[j] == table_s[q + 1, d]
                index = jnp.where(eq, within[j] + 24 * q, index)
                hit = hit | eq
            moved = jnp.take_along_axis(value, index, axis=1)
            result.append(jnp.where(hit, moved, 0.0))
        return result

    def add(g, carry):
        terms = [spread(4 * g + u) for u in range(4)]
        for u in range(4):
            joined = plan_s[1, 4 * g + u].astype(jnp.float32)
            carry = tuple(c * joined + v for c, v in zip(carry, terms[u]))
            for j in range(blocks):
                running[4 * g + u, :, 128 * j : 128 * (j + 1)] = carry[j]
        return carry

    zero = jnp.zeros((rows, 128), jnp.float32)
    lax.fori_loop(0, DEVICES // 4, add, (zero,) * blocks)

    diagonal = lax.broadcasted_iota(jnp.int32, (rows, 128), 1) == lax.broadcasted_iota(
        jnp.int32, (rows, 128), 0
    )

    def encode(s):
        t = plus(me, s)
        value = running[plan_s[2, t]] * plan_s[3, t].astype(jnp.float32)
        top = jnp.maximum(jnp.max(jnp.abs(value), axis=1, keepdims=True), FLOOR)
        coded = jnp.round(value * (LEVELS / top))
        outgoing[t] = coded.astype(jnp.int32).astype(jnp.int16)
        outscale[t] = jnp.sum(jnp.where(diagonal, top * (1.0 / LEVELS), 0.0), axis=0, keepdims=True)

    def post(s):
        t = plus(me, s)
        push(outscale, scales, t, send.at[4], recv.at[3])
        push(outgoing, arrived, t, send.at[3], recv.at[2])

    pipelined(encode, post)
    keep(outgoing, arrived, recv.at[2])
    keep(outscale, scales, recv.at[3])

    wait_rows(ask, others, send.at[0])
    wait_rows(stage, others, send.at[1])
    wait_rows(payload, others, send.at[2])
    wait_rows(outgoing, others, send.at[3])
    wait_rows(outscale, others, send.at[4])
    wait_rows(arrived, DEVICES, recv.at[2])
    wait_rows(scales, DEVICES, recv.at[3])


def decode_kernel(arrived, scales, out):
    rows = out.shape[1]
    diagonal = lax.broadcasted_iota(jnp.int32, (rows, 128), 1) == lax.broadcasted_iota(
        jnp.int32, (rows, 128), 0
    )

    @pl.loop(0, out.shape[0], unroll=4)
    def _(i):
        scale = jnp.sum(jnp.where(diagonal, scales[i], 0.0), axis=1, keepdims=True)
        out[i] = arrived[i].astype(jnp.int32).astype(jnp.float32) * scale


def per_device(prolong, stiffness, request, col_slot, col_pos, coarse_owner):
    slots, per_row, dof, _ = stiffness.shape
    vectors = prolong.shape[1]
    cols = 16 * vectors
    vmem = pl.BlockSpec(memory_space=pltpu.VMEM)
    smem = pl.BlockSpec(memory_space=pltpu.SMEM)
    arrived, scales = pl.pallas_call(
        exchange_kernel,
        out_shape=(
            jax.ShapeDtypeStruct((slots, vectors, cols), jnp.int16),
            jax.ShapeDtypeStruct((slots, 1, 128), jnp.float32),
        ),
        in_specs=[smem, smem, smem, vmem, vmem, pl.BlockSpec(memory_space=pl.ANY)],
        out_specs=(vmem, vmem),
        scratch_shapes=[
            pltpu.VMEM((slots, per_row, dof, dof), jnp.bfloat16),
            pltpu.VMEM((slots, 1, 128), jnp.int32),
            pltpu.VMEM((slots, 1, 128), jnp.int32),
            pltpu.VMEM((8, 128), jnp.int32),
            pltpu.SMEM((8, 128), jnp.int32),
            pltpu.VMEM((slots, vectors, dof), jnp.bfloat16),
            pltpu.VMEM((slots, vectors, dof), jnp.bfloat16),
            pltpu.VMEM((slots, vectors, dof), jnp.float32),
            pltpu.VMEM((slots, 2 * per_row * vectors, dof), jnp.bfloat16),
            pltpu.VMEM((slots, vectors, 128), jnp.int16),
            pltpu.VMEM((slots, vectors, 128), jnp.int16),
            pltpu.VMEM((8, 128), jnp.int32),
            pltpu.SMEM((8, 128), jnp.int32),
            pltpu.VMEM((slots, vectors, cols), jnp.float32),
            pltpu.VMEM((slots, vectors, cols), jnp.int16),
            pltpu.VMEM((slots, 1, 128), jnp.float32),
            pltpu.SemaphoreType.DMA,
            pltpu.SemaphoreType.DMA((2,)),
            pltpu.SemaphoreType.DMA((5,)),
            pltpu.SemaphoreType.DMA((4,)),
            pltpu.SemaphoreType.DMA((slots // GROUP,)),
        ],
        compiler_params=pltpu.CompilerParams(
            collective_id=0, has_side_effects=True, vmem_limit_bytes=60 * 1024 * 1024
        ),
        name="galerkin_exchange",
    )(request, col_slot.T, col_pos.T, coarse_owner.T, prolong, stiffness)
    step = GROUP
    return pl.pallas_call(
        decode_kernel,
        out_shape=jax.ShapeDtypeStruct((slots, vectors, cols), jnp.float32),
        grid=(slots // step,),
        in_specs=[
            pl.BlockSpec((step, vectors, cols), lambda i: (i, 0, 0)),
            pl.BlockSpec((step, 1, 128), lambda i: (i, 0, 0)),
        ],
        out_specs=pl.BlockSpec((step, vectors, cols), lambda i: (i, 0, 0)),
        name="decode",
    )(arrived, scales)


def solution(mesh):
    placed = (
        P(("gx", "gy"), None, None),
        P(("gx", "gy"), None, None, None),
        P(("gx", "gy")),
        P(("gx", "gy"), None),
        P(("gx", "gy"), None),
        P(("gx", "gy"), None),
    )
    return jax.shard_map(
        per_device,
        mesh=mesh,
        in_specs=placed,
        out_specs=P(("gx", "gy"), None, None),
        check_vma=False,
    )
```

time: 131 us -> 98.2 us (0.75)
  Pallas kernels: 129 us -> 98 us
  local copies, waits for them, and re-layouts: 1.34 us -> 0 us
    pallas_call x1, Pallas kernels: 122 us -> 90.5 us  [per_device(): pl.pallas_call(exchange_kernel, out_shape=(jax.ShapeDtypeStruct((slots, v...]
    broadcast_in_dim x1 -> x0, local copies, waits for them, and re-layouts: 1.34 us -> none  [per_device(): owner_b = jnp.broadcast_to(coarse_owner, (coarse_owner.shape[0], 128))]
where the time goes in v2:
time: 98.2 us; the launch traced here: 98 us
  Pallas kernels  98 us (100%)
    pallas_call x1, Pallas kernels, per_device(): pl.pallas_call(exchange_kernel, out_shape=(jax.ShapeDtypeStruct((slots, v...  90.5 us
    pallas_call x1, Pallas kernels, per_device(): pl.pallas_call(decode_kernel, out_shape=jax.ShapeDtypeStruct((slots, vect...  7.42 us

profile of v2, /device:TPU:1, one launch (start us, length us, event | category | flops | bytes accessed | tf_op | source)
XLA Modules:
  0.0 98.0 jit_solution(10629196588343905522)
XLA Ops:
  0.0 90.5 %galerkin_exchange.1 = (s16[128,24,384]{2,1,0:T(8,128)(2,1)}, f32[128,1,128]{2,1,0:T(1,128)}) custom-call(s32[128]{0:T(128)} %request.1, s32[4,128]{1,0:T(4,128)} %bitcast.3, s32[4,128]{1,0:T(4,128)} %bitcast.4, s32[1,64]{1,0:T(1,128)} %bitcast.5, bf16[64,24,128]{2,1,0:T(8,128)(2,1)} %prolong.1, bf16[128,4,128,128]{3,2,1,0:T(8,128)(2,1)} %stiffness.1), custom_call_target="tpu_custom_call" | custom-call | tf_op jit(solution)/shard_map/galerkin_exchange/pallas_call | solution.py:269
  90.5 7.4 %decode.1 = f32[128,24,384]{2,1,0:T(8,128)} custom-call(s16[128,24,384]{2,1,0:T(8,128)(2,1)} %get-tuple-element.7.arrived, f32[128,1,128]{2,1,0:T(1,128)} %get-tuple-element.8.scales), custom_call_target="tpu_custom_call" | custom-call | tf_op jit(solution)/shard_map/decode/pallas_call | solution.py:306

commit v3 on v2

--- a/solution.py
+++ b/solution.py
@@ -15,14 +15,23 @@
 TOP, LOW = 0b1011010, 0b0100101
 
 
-def plus(me, s):
-    o = (s * STRIDE) & (DEVICES - 1)
+def plus(me, o):
     return ((me & LOW) + (o & LOW)) ^ ((me ^ o) & TOP)
 
 
-def minus(me, s):
-    o = (s * STRIDE) & (DEVICES - 1)
+def minus(me, o):
     return ((me | TOP) - (o & LOW)) ^ ((me ^ ~o) & TOP)
+
+
+def mixed(s):
+    return (s * STRIDE) & (DEVICES - 1)
+
+
+def hops(o):
+    return sum(min(d, 4 - d) for d in (o >> 5, (o >> 2) & 3, o & 3))
+
+
+BY_HOPS = sorted((mixed(s) for s in range(1, DEVICES)), key=lambda o: -hops(o))
 
 
 def there(t):
@@ -35,25 +44,34 @@
 
 
 def exchange_kernel(
-    request, slot_of, pos_of, owner_row, prolong, stiffness,
+    request_in, slot_in, pos_in, owner_in, prolong_in, stiffness,
     arrived, scales,
+    request, slot_of, pos_of, owner_row, prolong,
     kbuf, ask, asked, table, table_s, stage, fetched_in, fetched, firsts, payload, partial_in,
-    plan, plan_s, running, outgoing, outscale,
-    ksem, local, send, recv, recv_block,
+    plan, plan_s, spread, running, outgoing, outscale,
+    ksem, load, local, send, recv, recv_block, recv_row,
 ):
     me = lax.axis_index("gx") * 16 + lax.axis_index("gy")
     rows, width = payload.shape[1], payload.shape[2]
     cols = outgoing.shape[2]
     others = DEVICES - 1
 
+    loads = [
+        pltpu.make_async_copy(source, target, load.at[k])
+        for k, (source, target) in enumerate(
+            ((request_in, request), (pos_in, pos_of), (slot_in, slot_of), (owner_in, owner_row), (prolong_in, prolong))
+        )
+    ]
+    for copy in loads:
+        copy.start()
     kcopy = pltpu.make_async_copy(stiffness, kbuf, ksem)
     kcopy.start()
 
     barrier = pltpu.get_barrier_semaphore()
-
-    @pl.loop(1, DEVICES)
-    def _(s):
-        pl.semaphore_signal(barrier, inc=1, device_id=there(plus(me, s)), device_id_type=MESH)
+    for o in BY_HOPS:
+        pl.semaphore_signal(barrier, inc=1, device_id=there(plus(me, o)), device_id_type=MESH)
+    for copy in loads:
+        copy.wait()
 
     lane1 = lax.broadcasted_iota(jnp.int32, (1, 128), 1)
 
@@ -79,9 +97,8 @@
     def keep(source, target, sem):
         pltpu.make_async_copy(source.at[me], target.at[me], sem).start()
 
-    @pl.loop(1, DEVICES)
-    def _(s):
-        push(ask, asked, plus(me, s), send.at[0], recv.at[0])
+    for o in BY_HOPS:
+        push(ask, asked, plus(me, o), send.at[0], recv.at[0])
 
     keep(ask, asked, recv.at[0])
     wait_rows(asked, DEVICES, recv.at[0])
@@ -95,9 +112,8 @@
     def _(d):
         stage[d] = prolong[table_s[0, d]]
 
-    @pl.loop(1, DEVICES)
-    def _(s):
-        push(stage, fetched_in, plus(me, s), send.at[1], recv_block.at[(s - 1) >> 4])
+    for s in range(1, DEVICES):
+        push(stage, fetched_in, plus(me, mixed(s)), send.at[1], recv_block.at[(s - 1) // GROUP])
 
     keep(stage, fetched_in, recv_block.at[DEVICES // GROUP - 1])
 
@@ -134,7 +150,7 @@
 
         @pl.loop(0, GROUP, unroll=4)
         def _(i):
-            t = minus(me, g * GROUP + i + 1)
+            t = minus(me, mixed(g * GROUP + i + 1))
             p = fetched_in[t]
             fetched[t] = p.astype(jnp.float32)
             pieces = []
@@ -147,7 +163,7 @@
     lane_p = lax.broadcasted_iota(jnp.int32, (rows, width), 1)
 
     def second(s):
-        t = plus(me, s)
+        t = plus(me, mixed(s))
         columns = [fetched[slot_of[q, t]] for q in range(4)]
         right = jnp.concatenate(columns + [jnp.zeros((32, 128), jnp.float32)], axis=0).astype(jnp.bfloat16)
         both = lax.dot_general(
@@ -180,21 +196,22 @@
         def _(s):
             post(s)
 
-    pipelined(second, lambda s: push(payload, partial_in, plus(me, s), send.at[2], recv.at[1]))
-    keep(payload, partial_in, recv.at[1])
-    plan_copy.wait()
-    wait_rows(partial_in, DEVICES, recv.at[1])
+    pipelined(
+        second,
+        lambda s: push(
+            payload, partial_in, plus(me, mixed(s)), send.at[2], recv_row.at[(s - 1) >> 4]
+        ),
+    )
+    keep(payload, partial_in, recv_row.at[DEVICES // GROUP - 1])
 
     lanes = [lax.broadcasted_iota(jnp.int32, (rows, 128), 1) + 128 * j for j in range(cols // 128)]
     column = [l // 24 for l in lanes]
     within = [l % 24 for l in lanes]
     blocks = cols // 128
 
-    def spread(i):
-        d = plan_s[0, i]
+    def place(d):
         got = partial_in[d].astype(jnp.int32).astype(jnp.float32)
         value = got * (jnp.exp2(got[:, 96:97]) * (1.0 / LEVELS))
-        result = []
         for j in range(blocks):
             index = jnp.zeros((rows, 128), jnp.int32)
             hit = jnp.zeros((rows, 128), jnp.bool_)
@@ -203,27 +220,35 @@
                 index = jnp.where(eq, within[j] + 24 * q, index)
                 hit = hit | eq
             moved = jnp.take_along_axis(value, index, axis=1)
-            result.append(jnp.where(hit, moved, 0.0))
-        return result
+            spread[d, :, 128 * j : 128 * (j + 1)] = jnp.where(hit, moved, 0.0)
+
+    @pl.loop(0, DEVICES // GROUP)
+    def _(g):
+        wait_rows(partial_in, GROUP, recv_row.at[g])
+
+        @pl.loop(0, GROUP // 4)
+        def _(i):
+            for u in range(4):
+                place(minus(me, mixed(g * GROUP + 4 * i + u + 1)))
+
+    plan_copy.wait()
 
     def add(g, carry):
-        terms = [spread(4 * g + u) for u in range(4)]
+        terms = [spread[plan_s[0, 4 * g + u]] for u in range(4)]
         for u in range(4):
             joined = plan_s[1, 4 * g + u].astype(jnp.float32)
-            carry = tuple(c * joined + v for c, v in zip(carry, terms[u]))
-            for j in range(blocks):
-                running[4 * g + u, :, 128 * j : 128 * (j + 1)] = carry[j]
+            carry = carry * joined + terms[u]
+            running[4 * g + u] = carry
         return carry
 
-    zero = jnp.zeros((rows, 128), jnp.float32)
-    lax.fori_loop(0, DEVICES // 4, add, (zero,) * blocks)
+    lax.fori_loop(0, DEVICES // 4, add, jnp.zeros((rows, cols), jnp.float32))
 
     diagonal = lax.broadcasted_iota(jnp.int32, (rows, 128), 1) == lax.broadcasted_iota(
         jnp.int32, (rows, 128), 0
     )
 
     def encode(s):
-        t = plus(me, s)
+        t = plus(me, mixed(s))
         value = running[plan_s[2, t]] * plan_s[3, t].astype(jnp.float32)
         top = jnp.maximum(jnp.max(jnp.abs(value), axis=1, keepdims=True), FLOOR)
         coded = jnp.round(value * (LEVELS / top))
@@ -231,33 +256,52 @@
         outscale[t] = jnp.sum(jnp.where(diagonal, top * (1.0 / LEVELS), 0.0), axis=0, keepdims=True)
 
     def post(s):
-        t = plus(me, s)
-        push(outscale, scales, t, send.at[4], recv.at[3])
-        push(outgoing, arrived, t, send.at[3], recv.at[2])
+        t = plus(me, mixed(s))
+        push(outscale, scales, t, send.at[4], recv.at[2])
+        push(outgoing, arrived, t, send.at[3], recv.at[1])
 
     pipelined(encode, post)
-    keep(outgoing, arrived, recv.at[2])
-    keep(outscale, scales, recv.at[3])
+    keep(outgoing, arrived, recv.at[1])
+    keep(outscale, scales, recv.at[2])
 
     wait_rows(ask, others, send.at[0])
     wait_rows(stage, others, send.at[1])
     wait_rows(payload, others, send.at[2])
     wait_rows(outgoing, others, send.at[3])
     wait_rows(outscale, others, send.at[4])
-    wait_rows(arrived, DEVICES, recv.at[2])
-    wait_rows(scales, DEVICES, recv.at[3])
-
-
-def decode_kernel(arrived, scales, out):
-    rows = out.shape[1]
+    wait_rows(arrived, DEVICES, recv.at[1])
+    wait_rows(scales, DEVICES, recv.at[2])
+
+
+def decode_kernel(arrived, scales_in, out, codes, scales, values, in_sem, scale_sem, out_sem):
+    rows = values.shape[1]
     diagonal = lax.broadcasted_iota(jnp.int32, (rows, 128), 1) == lax.broadcasted_iota(
         jnp.int32, (rows, 128), 0
     )
 
-    @pl.loop(0, out.shape[0], unroll=4)
-    def _(i):
-        scale = jnp.sum(jnp.where(diagonal, scales[i], 0.0), axis=1, keepdims=True)
-        out[i] = arrived[i].astype(jnp.int32).astype(jnp.float32) * scale
+    def copies(source, target, sem):
+        return [
+            pltpu.make_async_copy(source.at[pl.ds(c * GROUP, GROUP)], target.at[pl.ds(c * GROUP, GROUP)], sem.at[c])
+            for c in range(DEVICES // GROUP)
+        ]
+
+    reads, writes = copies(arrived, codes, in_sem), copies(values, out, out_sem)
+    scale_read = pltpu.make_async_copy(scales_in, scales, scale_sem)
+    scale_read.start()
+    for copy in reads:
+        copy.start()
+    scale_read.wait()
+    for c in range(DEVICES // GROUP):
+        reads[c].wait()
+
+        @pl.loop(c * GROUP, (c + 1) * GROUP, unroll=4)
+        def _(i):
+            scale = jnp.sum(jnp.where(diagonal, scales[i], 0.0), axis=1, keepdims=True)
+            values[i] = codes[i].astype(jnp.int32).astype(jnp.float32) * scale
+
+        writes[c].start()
+    for copy in writes:
+        copy.wait()
 
 
 def per_device(prolong, stiffness, request, col_slot, col_pos, coarse_owner):
@@ -265,16 +309,21 @@
     vectors = prolong.shape[1]
     cols = 16 * vectors
     vmem = pl.BlockSpec(memory_space=pltpu.VMEM)
-    smem = pl.BlockSpec(memory_space=pltpu.SMEM)
+    hbm = pl.BlockSpec(memory_space=pl.ANY)
     arrived, scales = pl.pallas_call(
         exchange_kernel,
         out_shape=(
             jax.ShapeDtypeStruct((slots, vectors, cols), jnp.int16),
             jax.ShapeDtypeStruct((slots, 1, 128), jnp.float32),
         ),
-        in_specs=[smem, smem, smem, vmem, vmem, pl.BlockSpec(memory_space=pl.ANY)],
-        out_specs=(vmem, vmem),
+        in_specs=[hbm] * 6,
+        out_specs=(hbm, hbm),
         scratch_shapes=[
+            pltpu.SMEM((slots,), jnp.int32),
+            pltpu.SMEM((per_row, slots), jnp.int32),
+            pltpu.SMEM((per_row, slots), jnp.int32),
+            pltpu.VMEM((1, coarse_owner.shape[0]), jnp.int32),
+            pltpu.VMEM(prolong.shape, jnp.bfloat16),
             pltpu.VMEM((slots, per_row, dof, dof), jnp.bfloat16),
             pltpu.VMEM((slots, 1, 128), jnp.int32),
             pltpu.VMEM((slots, 1, 128), jnp.int32),
@@ -289,12 +338,15 @@
             pltpu.VMEM((8, 128), jnp.int32),
             pltpu.SMEM((8, 128), jnp.int32),
             pltpu.VMEM((slots, vectors, cols), jnp.float32),
+            pltpu.VMEM((slots, vectors, cols), jnp.float32),
             pltpu.VMEM((slots, vectors, cols), jnp.int16),
             pltpu.VMEM((slots, 1, 128), jnp.float32),
             pltpu.SemaphoreType.DMA,
+            pltpu.SemaphoreType.DMA((5,)),
             pltpu.SemaphoreType.DMA((2,)),
             pltpu.SemaphoreType.DMA((5,)),
-            pltpu.SemaphoreType.DMA((4,)),
+            pltpu.SemaphoreType.DMA((3,)),
+            pltpu.SemaphoreType.DMA((slots // GROUP,)),
             pltpu.SemaphoreType.DMA((slots // GROUP,)),
         ],
         compiler_params=pltpu.CompilerParams(
@@ -302,16 +354,20 @@
         ),
         name="galerkin_exchange",
     )(request, col_slot.T, col_pos.T, coarse_owner.T, prolong, stiffness)
-    step = GROUP
     return pl.pallas_call(
         decode_kernel,
         out_shape=jax.ShapeDtypeStruct((slots, vectors, cols), jnp.float32),
-        grid=(slots // step,),
-        in_specs=[
-            pl.BlockSpec((step, vectors, cols), lambda i: (i, 0, 0)),
-            pl.BlockSpec((step, 1, 128), lambda i: (i, 0, 0)),
+        in_specs=[hbm, hbm],
+        out_specs=hbm,
+        scratch_shapes=[
+            pltpu.VMEM((slots, vectors, cols), jnp.int16),
+            pltpu.VMEM((slots, 1, 128), jnp.float32),
+            pltpu.VMEM((slots, vectors, cols), jnp.float32),
+            pltpu.SemaphoreType.DMA((slots // GROUP,)),
+            pltpu.SemaphoreType.DMA,
+            pltpu.SemaphoreType.DMA((slots // GROUP,)),
         ],
-        out_specs=pl.BlockSpec((step, vectors, cols), lambda i: (i, 0, 0)),
+        compiler_params=pltpu.CompilerParams(vmem_limit_bytes=60 * 1024 * 1024),
         name="decode",
     )(arrived, scales)
 

time: 98.2 us -> 86.7 us (0.88)
  Pallas kernels: 98 us -> 86.5 us
    pallas_call x1, Pallas kernels: 90.5 us -> 81.2 us  [per_device(): pl.pallas_call(exchange_kernel, out_shape=(jax.ShapeDtypeStruct((slots, v...]
    pallas_call x1, Pallas kernels: 7.42 us -> 5.29 us  [per_device(): pl.pallas_call(decode_kernel, out_shape=jax.ShapeDtypeStruct((slots, vect...]
where the time goes in v3:
time: 86.7 us; the launch traced here: 86.5 us
  Pallas kernels  86.5 us (100%)
    pallas_call x1, Pallas kernels, per_device(): pl.pallas_call(exchange_kernel, out_shape=(jax.ShapeDtypeStruct((slots, v...  81.2 us
    pallas_call x1, Pallas kernels, per_device(): pl.pallas_call(decode_kernel, out_shape=jax.ShapeDtypeStruct((slots, vect...  5.29 us

profile of v3, /device:TPU:1, one launch (start us, length us, event | category | flops | bytes accessed | tf_op | source)
XLA Modules:
  0.0 86.5 jit_solution(903529253442145003)
XLA Ops:
  0.0 81.2 %galerkin_exchange.1 = (s16[128,24,384]{2,1,0:T(8,128)(2,1)}, f32[128,1,128]{2,1,0:T(1,128)}) custom-call(s32[128]{0:T(128)} %request_in.1, s32[4,128]{1,0:T(4,128)} %bitcast.3, s32[4,128]{1,0:T(4,128)} %bitcast.4, s32[1,64]{1,0:T(1,128)} %bitcast.5, bf16[64,24,128]{2,1,0:T(8,128)(2,1)} %prolong_in.1, bf16[128,4,128,128]{3,2,1,0:T(8,128)(2,1)} %stiffness.1), custom_call_target="tpu_custom_call" | custom-call | tf_op jit(solution)/shard_map/galerkin_exchange/pallas_call | solution.py:313
  81.3 5.3 %decode.1 = f32[128,24,384]{2,1,0:T(8,128)} custom-call(s16[128,24,384]{2,1,0:T(8,128)(2,1)} %get-tuple-element.7.arrived, f32[128,1,128]{2,1,0:T(1,128)} %get-tuple-element.8.scales_in), custom_call_target="tpu_custom_call" | custom-call | tf_op jit(solution)/shard_map/decode/pallas_call | solution.py:357

commit v4 on v3

--- a/solution.py
+++ b/solution.py
@@ -11,6 +11,7 @@
 LEVELS = 32766.0
 FLOOR = 1e-30
 GROUP = 16
+STEPS = 8
 LAG = 2
 TOP, LOW = 0b1011010, 0b0100101
 
@@ -45,11 +46,11 @@
 
 def exchange_kernel(
     request_in, slot_in, pos_in, owner_in, prolong_in, stiffness,
-    arrived, scales,
+    result,
     request, slot_of, pos_of, owner_row, prolong,
     kbuf, ask, asked, table, table_s, stage, fetched_in, fetched, firsts, payload, partial_in,
-    plan, plan_s, spread, running, outgoing, outscale,
-    ksem, load, local, send, recv, recv_block, recv_row,
+    plan, plan_s, spread, running, outgoing, arrived, outscale, scales,
+    ksem, load, local, send, recv, recv_block, recv_row, recv_last, recv_scale,
 ):
     me = lax.axis_index("gx") * 16 + lax.axis_index("gy")
     rows, width = payload.shape[1], payload.shape[2]
@@ -174,9 +175,9 @@
             mine = both[2 * q * rows : (2 * q + 1) * rows] + both[(2 * q + 1) * rows : (2 * q + 2) * rows]
             value = jnp.where((lane_p >= 24 * q) & (lane_p < 24 * (q + 1)), mine, value)
         top = jnp.maximum(jnp.max(jnp.abs(value), axis=1, keepdims=True), FLOOR)
-        power = jnp.floor(jnp.log2(top)) + 1.0
-        coded = jnp.round(value * (jnp.exp2(-power) * LEVELS))
-        coded = jnp.where(lane_p >= 96, power, coded)
+        step = jnp.ceil(jnp.log2(top) * STEPS)
+        coded = jnp.round(value * (jnp.exp2(step * (-1.0 / STEPS)) * LEVELS))
+        coded = jnp.where(lane_p >= 96, step, coded)
         payload[t] = coded.astype(jnp.int32).astype(jnp.int16)
 
     def pipelined(make, post):
@@ -211,7 +212,7 @@
 
     def place(d):
         got = partial_in[d].astype(jnp.int32).astype(jnp.float32)
-        value = got * (jnp.exp2(got[:, 96:97]) * (1.0 / LEVELS))
+        value = got * (jnp.exp2(got[:, 96:97] * (1.0 / STEPS)) * (1.0 / LEVELS))
         for j in range(blocks):
             index = jnp.zeros((rows, 128), jnp.int32)
             hit = jnp.zeros((rows, 128), jnp.bool_)
@@ -251,56 +252,44 @@
         t = plus(me, mixed(s))
         value = running[plan_s[2, t]] * plan_s[3, t].astype(jnp.float32)
         top = jnp.maximum(jnp.max(jnp.abs(value), axis=1, keepdims=True), FLOOR)
-        coded = jnp.round(value * (LEVELS / top))
-        outgoing[t] = coded.astype(jnp.int32).astype(jnp.int16)
+        outgoing[t] = jnp.round(value * (LEVELS / top)).astype(jnp.int32).astype(jnp.int16)
         outscale[t] = jnp.sum(jnp.where(diagonal, top * (1.0 / LEVELS), 0.0), axis=0, keepdims=True)
 
     def post(s):
         t = plus(me, mixed(s))
-        push(outscale, scales, t, send.at[4], recv.at[2])
-        push(outgoing, arrived, t, send.at[3], recv.at[1])
+        push(outscale, scales, t, send.at[4], recv_scale.at[(s - 1) >> 4])
+        push(outgoing, arrived, t, send.at[3], recv_last.at[(s - 1) >> 4])
 
     pipelined(encode, post)
-    keep(outgoing, arrived, recv.at[1])
-    keep(outscale, scales, recv.at[2])
-
-    wait_rows(ask, others, send.at[0])
-    wait_rows(stage, others, send.at[1])
-    wait_rows(payload, others, send.at[2])
-    wait_rows(outgoing, others, send.at[3])
-    wait_rows(outscale, others, send.at[4])
-    wait_rows(arrived, DEVICES, recv.at[1])
-    wait_rows(scales, DEVICES, recv.at[2])
-
-
-def decode_kernel(arrived, scales_in, out, codes, scales, values, in_sem, scale_sem, out_sem):
-    rows = values.shape[1]
-    diagonal = lax.broadcasted_iota(jnp.int32, (rows, 128), 1) == lax.broadcasted_iota(
-        jnp.int32, (rows, 128), 0
-    )
-
-    def copies(source, target, sem):
-        return [
-            pltpu.make_async_copy(source.at[pl.ds(c * GROUP, GROUP)], target.at[pl.ds(c * GROUP, GROUP)], sem.at[c])
-            for c in range(DEVICES // GROUP)
-        ]
-
-    reads, writes = copies(arrived, codes, in_sem), copies(values, out, out_sem)
-    scale_read = pltpu.make_async_copy(scales_in, scales, scale_sem)
-    scale_read.start()
-    for copy in reads:
+    keep(outscale, scales, recv_scale.at[DEVICES // GROUP - 1])
+    keep(outgoing, arrived, recv_last.at[DEVICES // GROUP - 1])
+
+    @pl.loop(0, DEVICES // GROUP)
+    def _(g):
+        wait_rows(scales, GROUP, recv_scale.at[g])
+        wait_rows(arrived, GROUP, recv_last.at[g])
+
+        @pl.loop(0, GROUP // 4)
+        def _(i):
+            for u in range(4):
+                t = minus(me, mixed(g * GROUP + 4 * i + u + 1))
+                scale = jnp.sum(jnp.where(diagonal, scales[t], 0.0), axis=1, keepdims=True)
+                result[t] = arrived[t].astype(jnp.int32).astype(jnp.float32) * scale
+
+    for k, ref in enumerate((ask, stage, payload, outgoing, outscale)):
+        wait_rows(ref, others, send.at[k])
+
+
+def store_kernel(values, out, sem):
+    copies = [
+        pltpu.make_async_copy(
+            values.at[pl.ds(c * GROUP, GROUP)], out.at[pl.ds(c * GROUP, GROUP)], sem.at[c]
+        )
+        for c in range(DEVICES // GROUP)
+    ]
+    for copy in copies:
         copy.start()
-    scale_read.wait()
-    for c in range(DEVICES // GROUP):
-        reads[c].wait()
-
-        @pl.loop(c * GROUP, (c + 1) * GROUP, unroll=4)
-        def _(i):
-            scale = jnp.sum(jnp.where(diagonal, scales[i], 0.0), axis=1, keepdims=True)
-            values[i] = codes[i].astype(jnp.int32).astype(jnp.float32) * scale
-
-        writes[c].start()
-    for copy in writes:
+    for copy in copies:
         copy.wait()
 
 
@@ -310,14 +299,11 @@
     cols = 16 * vectors
     vmem = pl.BlockSpec(memory_space=pltpu.VMEM)
     hbm = pl.BlockSpec(memory_space=pl.ANY)
-    arrived, scales = pl.pallas_call(
+    result = pl.pallas_call(
         exchange_kernel,
-        out_shape=(
-            jax.ShapeDtypeStruct((slots, vectors, cols), jnp.int16),
-            jax.ShapeDtypeStruct((slots, 1, 128), jnp.float32),
-        ),
+        out_shape=pltpu.VMEM((slots, vectors, cols), jnp.float32),
         in_specs=[hbm] * 6,
-        out_specs=(hbm, hbm),
+        out_specs=vmem,
         scratch_shapes=[
             pltpu.SMEM((slots,), jnp.int32),
             pltpu.SMEM((per_row, slots), jnp.int32),
@@ -340,36 +326,33 @@
             pltpu.VMEM((slots, vectors, cols), jnp.float32),
             pltpu.VMEM((slots, vectors, cols), jnp.float32),
             pltpu.VMEM((slots, vectors, cols), jnp.int16),
+            pltpu.VMEM((slots, vectors, cols), jnp.int16),
+            pltpu.VMEM((slots, 1, 128), jnp.float32),
             pltpu.VMEM((slots, 1, 128), jnp.float32),
             pltpu.SemaphoreType.DMA,
             pltpu.SemaphoreType.DMA((5,)),
             pltpu.SemaphoreType.DMA((2,)),
             pltpu.SemaphoreType.DMA((5,)),
-            pltpu.SemaphoreType.DMA((3,)),
+            pltpu.SemaphoreType.DMA((1,)),
+            pltpu.SemaphoreType.DMA((slots // GROUP,)),
+            pltpu.SemaphoreType.DMA((slots // GROUP,)),
             pltpu.SemaphoreType.DMA((slots // GROUP,)),
             pltpu.SemaphoreType.DMA((slots // GROUP,)),
         ],
         compiler_params=pltpu.CompilerParams(
-            collective_id=0, has_side_effects=True, vmem_limit_bytes=60 * 1024 * 1024
+            collective_id=0, has_side_effects=True, vmem_limit_bytes=56 * 1024 * 1024
         ),
         name="galerkin_exchange",
     )(request, col_slot.T, col_pos.T, coarse_owner.T, prolong, stiffness)
     return pl.pallas_call(
-        decode_kernel,
+        store_kernel,
         out_shape=jax.ShapeDtypeStruct((slots, vectors, cols), jnp.float32),
-        in_specs=[hbm, hbm],
+        in_specs=[vmem],
         out_specs=hbm,
-        scratch_shapes=[
-            pltpu.VMEM((slots, vectors, cols), jnp.int16),
-            pltpu.VMEM((slots, 1, 128), jnp.float32),
-            pltpu.VMEM((slots, vectors, cols), jnp.float32),
-            pltpu.SemaphoreType.DMA((slots // GROUP,)),
-            pltpu.SemaphoreType.DMA,
-            pltpu.SemaphoreType.DMA((slots // GROUP,)),
-        ],
-        compiler_params=pltpu.CompilerParams(vmem_limit_bytes=60 * 1024 * 1024),
-        name="decode",
-    )(arrived, scales)
+        scratch_shapes=[pltpu.SemaphoreType.DMA((slots // GROUP,))],
+        compiler_params=pltpu.CompilerParams(vmem_limit_bytes=16 * 1024 * 1024),
+        name="store",
+    )(result)
 
 
 def solution(mesh):

time: 86.7 us -> 84 us (0.969)
  Pallas kernels: 86.5 us -> 83.9 us
    pallas_call x2, Pallas kernels: 86.5 us -> 83.9 us  [the longest x1 81.6 us: per_device(): pl.pallas_call(exchange_kernel, out_shape=pltpu.VMEM((slots, vectors, col...]
where the time goes in v4:
time: 84 us; the launch traced here: 83.9 us
  Pallas kernels  83.9 us (100%)
    pallas_call x1, Pallas kernels, per_device(): pl.pallas_call(exchange_kernel, out_shape=pltpu.VMEM((slots, vectors, col...  81.6 us
    pallas_call x1, Pallas kernels, per_device(): pl.pallas_call(store_kernel, out_shape=jax.ShapeDtypeStruct((slots, vecto...  2.24 us

profile of v4, /device:TPU:1, one launch (start us, length us, event | category | flops | bytes accessed | tf_op | source)
XLA Modules:
  0.0 83.9 jit_solution(2928614189449882575)
XLA Ops:
  0.0 81.6 %galerkin_exchange.1.values = f32[128,24,384]{2,1,0:T(8,128)S(1)} custom-call(s32[128]{0:T(128)} %request_in.1, s32[4,128]{1,0:T(4,128)} %bitcast.3, s32[4,128]{1,0:T(4,128)} %bitcast.4, s32[1,64]{1,0:T(1,128)} %bitcast.5, bf16[64,24,128]{2,1,0:T(8,128)(2,1)} %prolong_in.1, bf16[128,4,128,128]{3,2,1,0:T(8,128)(2,1)} %stiffness.1), custom_call_target="tpu_custom_call" | custom-call | tf_op jit(solution)/shard_map/galerkin_exchange/pallas_call | solution.py:302
  81.6 2.2 %store.1 = f32[128,24,384]{2,1,0:T(8,128)} custom-call(f32[128,24,384]{2,1,0:T(8,128)S(1)} %galerkin_exchange.1.values), custom_call_target="tpu_custom_call" | custom-call | tf_op jit(solution)/shard_map/store/pallas_call | solution.py:347

commit v5 on v4

--- a/solution.py
+++ b/solution.py
@@ -7,12 +7,12 @@
 
 MESH = pl.DeviceIdType.MESH
 DEVICES = 128
-STRIDE = 37
+STRIDE = 53
 LEVELS = 32766.0
 FLOOR = 1e-30
-GROUP = 16
+GROUP = 8
 STEPS = 8
-LAG = 2
+LAG = 1
 TOP, LOW = 0b1011010, 0b0100101
 
 
@@ -200,7 +200,7 @@
     pipelined(
         second,
         lambda s: push(
-            payload, partial_in, plus(me, mixed(s)), send.at[2], recv_row.at[(s - 1) >> 4]
+            payload, partial_in, plus(me, mixed(s)), send.at[2], recv_row.at[(s - 1) >> 3]
         ),
     )
     keep(payload, partial_in, recv_row.at[DEVICES // GROUP - 1])
@@ -257,8 +257,8 @@
 
     def post(s):
         t = plus(me, mixed(s))
-        push(outscale, scales, t, send.at[4], recv_scale.at[(s - 1) >> 4])
-        push(outgoing, arrived, t, send.at[3], recv_last.at[(s - 1) >> 4])
+        push(outscale, scales, t, send.at[4], recv_scale.at[(s - 1) >> 3])
+        push(outgoing, arrived, t, send.at[3], recv_last.at[(s - 1) >> 3])
 
     pipelined(encode, post)
     keep(outscale, scales, recv_scale.at[DEVICES // GROUP - 1])

time: 84 us -> 83 us (0.988)
  Pallas kernels: 83.9 us -> 82.9 us
    pallas_call x1, Pallas kernels: 81.6 us -> 80.6 us  [per_device(): pl.pallas_call(exchange_kernel, out_shape=pltpu.VMEM((slots, vectors, col...]
where the time goes in v5:
time: 83 us; the launch traced here: 82.9 us
  Pallas kernels  82.9 us (100%)
    pallas_call x1, Pallas kernels, per_device(): pl.pallas_call(exchange_kernel, out_shape=pltpu.VMEM((slots, vectors, col...  80.6 us
    pallas_call x1, Pallas kernels, per_device(): pl.pallas_call(store_kernel, out_shape=jax.ShapeDtypeStruct((slots, vecto...  2.31 us

profile of v5, /device:TPU:1, one launch (start us, length us, event | category | flops | bytes accessed | tf_op | source)
XLA Modules:
  0.0 82.9 jit_solution(16223341975407685132)
XLA Ops:
  0.0 80.6 %galerkin_exchange.1.values = f32[128,24,384]{2,1,0:T(8,128)S(1)} custom-call(s32[128]{0:T(128)} %request_in.1, s32[4,128]{1,0:T(4,128)} %bitcast.3, s32[4,128]{1,0:T(4,128)} %bitcast.4, s32[1,64]{1,0:T(1,128)} %bitcast.5, bf16[64,24,128]{2,1,0:T(8,128)(2,1)} %prolong_in.1, bf16[128,4,128,128]{3,2,1,0:T(8,128)(2,1)} %stiffness.1), custom_call_target="tpu_custom_call" | custom-call | tf_op jit(solution)/shard_map/galerkin_exchange/pallas_call | solution.py:302
  80.6 2.3 %store.1 = f32[128,24,384]{2,1,0:T(8,128)} custom-call(f32[128,24,384]{2,1,0:T(8,128)S(1)} %galerkin_exchange.1.values), custom_call_target="tpu_custom_call" | custom-call | tf_op jit(solution)/shard_map/store/pallas_call | solution.py:347

commit v6 on v5

--- a/solution.py
+++ b/solution.py
@@ -149,7 +149,7 @@
     def _(g):
         wait_rows(fetched_in, GROUP, recv_block.at[g])
 
-        @pl.loop(0, GROUP, unroll=4)
+        @pl.loop(0, GROUP, unroll=8)
         def _(i):
             t = minus(me, mixed(g * GROUP + i + 1))
             p = fetched_in[t]
@@ -227,10 +227,8 @@
     def _(g):
         wait_rows(partial_in, GROUP, recv_row.at[g])
 
-        @pl.loop(0, GROUP // 4)
-        def _(i):
-            for u in range(4):
-                place(minus(me, mixed(g * GROUP + 4 * i + u + 1)))
+        for u in range(GROUP):
+            place(minus(me, mixed(g * GROUP + u + 1)))
 
     plan_copy.wait()
 
@@ -269,12 +267,10 @@
         wait_rows(scales, GROUP, recv_scale.at[g])
         wait_rows(arrived, GROUP, recv_last.at[g])
 
-        @pl.loop(0, GROUP // 4)
-        def _(i):
-            for u in range(4):
-                t = minus(me, mixed(g * GROUP + 4 * i + u + 1))
-                scale = jnp.sum(jnp.where(diagonal, scales[t], 0.0), axis=1, keepdims=True)
-                result[t] = arrived[t].astype(jnp.int32).astype(jnp.float32) * scale
+        for u in range(GROUP):
+            t = minus(me, mixed(g * GROUP + u + 1))
+            scale = jnp.sum(jnp.where(diagonal, scales[t], 0.0), axis=1, keepdims=True)
+            result[t] = arrived[t].astype(jnp.int32).astype(jnp.float32) * scale
 
     for k, ref in enumerate((ask, stage, payload, outgoing, outscale)):
         wait_rows(ref, others, send.at[k])

time: 83 us -> 81.4 us (0.981)
  Pallas kernels: 82.9 us -> 81.3 us
    pallas_call x1, Pallas kernels: 80.6 us -> 79 us  [per_device(): pl.pallas_call(exchange_kernel, out_shape=pltpu.VMEM((slots, vectors, col...]
where the time goes in v6:
time: 81.4 us; the launch traced here: 81.3 us
  Pallas kernels  81.3 us (100%)
    pallas_call x1, Pallas kernels, per_device(): pl.pallas_call(exchange_kernel, out_shape=pltpu.VMEM((slots, vectors, col...  79 us
    pallas_call x1, Pallas kernels, per_device(): pl.pallas_call(store_kernel, out_shape=jax.ShapeDtypeStruct((slots, vecto...  2.31 us

profile of v6, /device:TPU:1, one launch (start us, length us, event | category | flops | bytes accessed | tf_op | source)
XLA Modules:
  0.0 81.3 jit_solution(13331278805288656763)
XLA Ops:
  0.0 79.0 %galerkin_exchange.1.values = f32[128,24,384]{2,1,0:T(8,128)S(1)} custom-call(s32[128]{0:T(128)} %request_in.1, s32[4,128]{1,0:T(4,128)} %bitcast.3, s32[4,128]{1,0:T(4,128)} %bitcast.4, s32[1,64]{1,0:T(1,128)} %bitcast.5, bf16[64,24,128]{2,1,0:T(8,128)(2,1)} %prolong_in.1, bf16[128,4,128,128]{3,2,1,0:T(8,128)(2,1)} %stiffness.1), custom_call_target="tpu_custom_call" | custom-call | tf_op jit(solution)/shard_map/galerkin_exchange/pallas_call | solution.py:298
  79.0 2.3 %store.1 = f32[128,24,384]{2,1,0:T(8,128)} custom-call(f32[128,24,384]{2,1,0:T(8,128)S(1)} %galerkin_exchange.1.values), custom_call_target="tpu_custom_call" | custom-call | tf_op jit(solution)/shard_map/store/pallas_call | solution.py:343
